TPU v7x, 256 devices: a whole 4x4x8 slice. The times are simulated.
256 devices in a mesh: grp: 32 (over z, y), rep: 8 (over x, core).
Axes of the slice: x: 4, y: 4, z: 8, core: 2. Of those that a mesh axis runs over, the one named last changes fastest.
Arguments:
- queries: bfloat16 [64, 8, 32, 128], P('grp', 'rep'), may hold values from -3.2 to 3.2
- passages: bfloat16 [2048, 8, 180, 128], P('grp', 'rep'), may hold values from -1.796875 to 1.796875
- lengths: int32 [2048, 8], P('grp', 'rep'), may hold values from 16 to 180
- cand_ids: int32 [64, 8, 64], P('grp', 'rep'), may hold values from 0 to 2047, as said below
- owner_map: int32 [8, 2048], P('rep'), may hold values from 0 to 2047, as said below
- teacher: float32 [64, 8, 64], P('grp', 'rep'), may hold values from -12 to 312
- weights: float32 [64, 8], P('grp', 'rep'), may hold values from 0.5 to 18
Outputs:
- loss: float32 [], replicated
- query_grad: float32 [64, 8, 32, 128], P('grp', 'rep')
- passage_grad: bfloat16 [2048, 8, 180, 128], P('grp', 'rep')
Inputs may be any that keep to these rules, and one draw needn't show every extreme that they name: `cand_ids`: within each replica, the 128 candidates of the queries of one grp index have storage rows of which at most 8 (counted with repeats) lie in any one aligned block of 64 rows; in every draw, in each replica, one block receives exactly 8 from every grp index. `owner_map`: each row is a permutation of 0 to 2047.
All inputs are finite; a program needn't handle non-finite values.
Results may differ from a plain program's by a relative error of at most 0.0055.
Values may be sent and summed in bfloat16 or wider, within the bound.
A program may use at most 128 MiB of HBM per device.

v0:
```python
import jax
import jax.numpy as jnp
from jax import lax
from jax.sharding import Mesh
from jax.sharding import PartitionSpec as P

GRP = ("grp_0", "grp_1")
REP = ("rep_0", "rep_1")
GRP_REP = ("grp_0", "grp_1", "rep_0", "rep_1")
temper = 0.05


def over_axes(shard, axes):
    for axis in axes:
        shard = lax.psum(shard, axis)
    return shard


def token_softmax(products, lengths_used):
    usable = (
        lax.broadcasted_iota(jnp.int32, products.shape, products.ndim - 1)
        < lengths_used[..., None, None]
    )
    scaled = jnp.where(usable, products / temper, -1e30)
    highest = jnp.max(scaled, axis=-1, keepdims=True)
    powers = jnp.where(usable, jnp.exp(scaled - highest), 0.0)
    summed = jnp.sum(powers, axis=-1, keepdims=True)
    matched = temper * (highest[..., 0] + jnp.log(summed[..., 0]))
    return (matched, powers / summed)


def on_device(queries, passages, lengths, cand_ids, owner_map, teacher, weights):
    groups = lax.axis_size(GRP)
    replicas = lax.axis_size(REP)
    query_local = queries.shape[0]
    query_len = queries.shape[2]
    feature_dim = queries.shape[3]
    passage_local = passages.shape[0]
    token_len = passages.shape[2]
    candidates = cand_ids.shape[2]
    ref_count = query_local * candidates
    capacity = 2 * ref_count // groups
    slot_count = groups * capacity
    block_width = token_len * feature_dim
    query_width = query_len * feature_dim
    position_table = owner_map[0]
    wanted = cand_ids[:, 0, :].reshape(ref_count)
    table_index = jnp.arange(position_table.shape[0], dtype=jnp.int32)
    positions = jnp.sum(
        jnp.where(wanted[:, None] == table_index[None, :], position_table[None, :], 0), axis=1
    )
    owner_index = positions // passage_local
    local_row = positions % passage_local
    owner_hot = (owner_index[:, None] == jnp.arange(groups, dtype=jnp.int32)[None, :]).astype(
        jnp.int32
    )
    before = jnp.cumsum(owner_hot, axis=0) - owner_hot
    slot_rank = jnp.sum(before * owner_hot, axis=1)
    slot_index = owner_index * capacity + slot_rank
    request = jnp.full((slot_count,), -1, jnp.int32).at[slot_index].set(local_row)
    asked_rows = lax.all_to_all(
        request.reshape(groups, capacity), GRP, split_axis=0, concat_axis=0, tiled=True
    ).reshape(slot_count)
    present = asked_rows >= 0
    safe_rows = jnp.maximum(asked_rows, 0)
    slot_lengths = jnp.where(present, lengths[:, 0][safe_rows], 0)
    stored_index = jnp.arange(passage_local, dtype=jnp.int32)
    gather_hot = (asked_rows[None, :] == stored_index[:, None]).astype(jnp.bfloat16)
    pick_hot = (asked_rows[:, None] == stored_index[None, :]).astype(jnp.bfloat16)
    route_hot = (slot_index[:, None] == jnp.arange(slot_count, dtype=jnp.int32)[None, :]).astype(
        jnp.bfloat16
    )
    flat_passages = passages.reshape(passage_local, block_width)
    query_flat = queries[:, 0]
    query_weights = weights[:, 0]
    query_source = jnp.arange(ref_count, dtype=jnp.int32) // candidates
    blocks_flat = jnp.dot(pick_hot, flat_passages, preferred_element_type=jnp.float32).astype(
        jnp.bfloat16
    )
    ref_queries = query_flat[query_source].reshape(ref_count, query_width)
    slot_queries = jnp.einsum(
        "rs,rk->sk", route_hot, ref_queries, preferred_element_type=jnp.float32
    ).astype(jnp.bfloat16)
    got_queries = lax.all_to_all(
        slot_queries.reshape(groups, capacity, query_width),
        GRP,
        split_axis=0,
        concat_axis=0,
        tiled=True,
    )
    got_queries = got_queries.reshape(slot_count, query_len, feature_dim)
    blocks = blocks_flat.reshape(slot_count, token_len, feature_dim)
    products = jnp.einsum("sid,sjd->sij", got_queries, blocks, preferred_element_type=jnp.float32)
    matched, attention = token_softmax(products, jnp.maximum(slot_lengths, 1))
    slot_scores = jnp.sum(matched, axis=-1)
    back_scores = lax.all_to_all(
        slot_scores.reshape(groups, capacity), GRP, split_axis=0, concat_axis=0, tiled=True
    ).reshape(slot_count)
    student = back_scores[slot_index].reshape(query_local, candidates)
    log_student = jax.nn.log_softmax(student, axis=-1)
    log_teacher = jax.nn.log_softmax(teacher[:, 0], axis=-1)
    teacher_prob = jnp.exp(log_teacher)
    divergence = jnp.sum(teacher_prob * (log_teacher - log_student), axis=-1)
    totals = (
        over_axes(jnp.sum(query_weights * divergence), GRP_REP),
        over_axes(jnp.sum(query_weights), GRP_REP),
    )
    loss_value = totals[0] / totals[1]
    scale_all = query_local * groups * replicas
    score_grad = (
        scale_all * query_weights[:, None] / totals[1] * (jnp.exp(log_student) - teacher_prob)
    )
    loss_value, score_grad = (loss_value, score_grad)
    slot_score_grad = (
        jnp.zeros((slot_count,), jnp.float32).at[slot_index].set(score_grad.reshape(ref_count))
    )
    arrived = lax.all_to_all(
        slot_score_grad.reshape(groups, capacity), GRP, split_axis=0, concat_axis=0, tiled=True
    ).reshape(slot_count)
    scaled_grad = (arrived[:, None, None] * attention).astype(jnp.bfloat16)
    pair_query = jnp.einsum(
        "sij,sjd->sid", scaled_grad, blocks, preferred_element_type=jnp.float32
    ).astype(jnp.bfloat16)
    returned_queries = lax.all_to_all(
        pair_query.reshape(groups, capacity, query_width),
        GRP,
        split_axis=0,
        concat_axis=0,
        tiled=True,
    )
    ordered = jnp.dot(
        route_hot,
        returned_queries.reshape(slot_count, query_width),
        preferred_element_type=jnp.float32,
    )
    query_grad = jnp.sum(ordered.reshape(query_local, candidates, query_len, feature_dim), axis=1)
    returned = jnp.einsum(
        "sij,sid->sjd", scaled_grad, got_queries, preferred_element_type=jnp.float32
    ).astype(jnp.bfloat16)
    returned = returned.reshape(slot_count, block_width)
    passage_sum = jnp.dot(gather_hot, returned, preferred_element_type=jnp.float32)
    passage_grad = passage_sum.astype(jnp.bfloat16).reshape(
        passage_local, 1, token_len, feature_dim
    )
    return (loss_value, query_grad[:, None], passage_grad)


def solution(mesh):
    finer = Mesh(mesh.devices.reshape(8, 4, 4, 2), ("grp_0", "grp_1", "rep_0", "rep_1"))
    in_specs = (
        P(GRP, REP, None, None),
        P(GRP, REP, None, None),
        P(GRP, REP),
        P(GRP, REP, None),
        P(REP, None),
        P(GRP, REP, None),
        P(GRP, REP),
    )
    out_specs = (P(), P(GRP, REP, None, None), P(GRP, REP, None, None))
    return jax.shard_map(
        on_device, mesh=finer, in_specs=in_specs, out_specs=out_specs, check_vma=False
    )
```

profile of v0, /device:TPU:8, one launch (start us, length us, event | category | flops | bytes accessed | tf_op | source)
XLA Modules:
  0.0 256.7 jit_solution(11497343918002270158)
XLA Ops:
  5.7 11.7 %all-to-all-start = ((s32[32,1,8]{2,1,0:T(1,128)}), s32[32,1,8]{2,1,0:T(1,128)S(1)}, u32[]{:S(2)}, u32[]{:S(2)}) async-start(s32[32,1,8]{2,1,0:T(1,128)} %bitcast.6), calls=%async_computation | async-start | bytes 32768 | tf_op jit(solution)/shard_map/all_to_all | solution.py:61
  20.4 5.5 %all-to-all-done = s32[32,1,8]{2,1,0:T(1,128)S(1)} async-done(((s32[32,1,8]{2,1,0:T(1,128)}), s32[32,1,8]{2,1,0:T(1,128)S(1)}, u32[]{:S(2)}, u32[]{:S(2)}) %all-to-all-start) | async-done | bytes 1056 | tf_op jit(solution)/shard_map/all_to_all | solution.py:61
  25.9 5.8 %all-to-all-start.1 = ((bf16[32,8,4096]{2,1,0:T(8,128)(2,1)}), bf16[32,8,4096]{2,1,0:T(8,128)(2,1)}, u32[]{:S(2)}, u32[]{:S(2)}) async-start(bf16[32,8,4096]{2,1,0:T(8,128)(2,1)} %fusion.1), calls=%async_computation.1 | async-start | bytes 4194304 | tf_op jit(solution)/shard_map/all_to_all | solution.py:84
  31.7 3.7 %copy.30 = bf16[64,1,180,128]{3,2,0,1:T(8,128)(2,1)S(1)} copy(bf16[64,1,180,128]{3,0,2,1:T(8,128)(2,1)} %param.9) | data formatting | bytes 5898240 | tf_op args[1]
  36.7 6.2 %convolution_convert_fusion = bf16[256,23040]{1,0:T(8,128)(2,1)} fusion(bf16[8,8,180,128]{3,2,1,0:T(8,128)(2,1)S(1)} %bitcast.71, s32[256]{0:T(256)S(1)} %reshape.239), kind=kOutput, calls=%fused_computation.5 | convolution fusion | flops 760889344 | bytes 14746624 | tf_op jit(solution)/shard_map/dot_general | solution.py:77
  42.9 16.2 %copy.31 = bf16[256,23040]{0,1:T(8,128)(2,1)} copy(bf16[256,23040]{1,0:T(8,128)(2,1)} %convolution_convert_fusion) | data formatting | bytes 23592960 | tf_op jit(solution)/shard_map/convert_element_type | solution.py:77
  59.1 16.5 %copy.32 = bf16[256,180,128]{2,1,0:T(8,128)(2,1)} copy(bf16[256,180,128]{0,2,1:T(8,128)(2,1)} %bitcast.70) | data formatting | bytes 23592960 | tf_op jit(solution)/shard_map/reshape | solution.py:92
  82.4 15.2 %fusion = (f32[256,32]{1,0:T(8,128)S(1)}, f32[256,32,180]{2,1,0:T(8,128)}) fusion(s32[256]{0:T(256)S(1)} %fusion.14, bf16[256,32,128]{2,1,0:T(8,128)(2,1)S(1)} %bitcast.73, bf16[256,180,128]{2,1,0:T(8,128)(2,1)} %copy.32), kind=kOutput, calls=%fused_computation.12 | convolution fusion | flops 383377408 | bytes 19825664 | tf_op jit(solution)/shard_map/sid,sjd->sij/dot_general | solution.py:93
  97.7 6.4 %fusion.2 = f32[256,32]{1,0:T(8,128)S(1)} fusion(f32[256,32,180]{2,1,0:T(8,128)} %get-tuple-element.29, f32[256,32]{1,0:T(8,128)S(1)} %get-tuple-element.28, s32[256]{0:T(256)S(1)} %fusion.14), kind=kLoop, calls=%fused_computation.15 | loop fusion | flops 8839168 | bytes 5964800 | tf_op jit(solution)/shard_map/reduce_sum | solution.py:27
  104.9 7.1 %all-to-all-start.2 = ((f32[32,1,8]{2,1,0:T(1,128)}), f32[32,1,8]{2,1,0:T(1,128)S(1)}, u32[]{:S(2)}, u32[]{:S(2)}) async-start(f32[32,1,8]{2,1,0:T(1,128)} %bitcast.12), calls=%async_computation.2 | async-start | bytes 32768 | tf_op jit(solution)/shard_map/all_to_all | solution.py:96
  112.7 7.8 %all-to-all-done.2 = f32[32,1,8]{2,1,0:T(1,128)S(1)} async-done(((f32[32,1,8]{2,1,0:T(1,128)}), f32[32,1,8]{2,1,0:T(1,128)S(1)}, u32[]{:S(2)}, u32[]{:S(2)}) %all-to-all-start.2) | async-done | bytes 1056 | tf_op jit(solution)/shard_map/all_to_all | solution.py:96
  124.3 15.4 %all-reduce = (f32[]{:T(128)}, f32[]{:T(128)}) all-reduce(f32[]{:T(128)} %fusion.17, f32[]{:T(128)} %reduce_sum.97), channel_id=1, replica_groups=mesh['grp_0'=8,'grp_1'=4,'rep_0'=4,'rep_1'=2] {'grp_0'}, use_global_device_ids=true, to_apply=%region_11.13 | all-reduce | flops 2 | bytes 16 | tf_op jit(solution)/shard_map/psum | solution.py:15
  139.7 9.9 %all-reduce.2 = (f32[]{:T(128)}, f32[]{:T(128)}) all-reduce(f32[]{:T(128)} %get-tuple-element.18, f32[]{:T(128)} %get-tuple-element.19), channel_id=1, replica_groups=mesh['grp_0'=8,'grp_1'=4,'rep_0'=4,'rep_1'=2] {'grp_1'}, use_global_device_ids=true, to_apply=%region_12.14 | all-reduce | flops 2 | bytes 16 | tf_op jit(solution)/shard_map/psum | solution.py:15
  149.5 11.0 %all-reduce.1 = (f32[]{:T(128)}, f32[]{:T(128)}) all-reduce(f32[]{:T(128)} %get-tuple-element.22, f32[]{:T(128)} %get-tuple-element.23), channel_id=1, replica_groups=mesh['grp_0'=8,'grp_1'=4,'rep_0'=4,'rep_1'=2] {'rep_0'}, use_global_device_ids=true, to_apply=%region_13.15 | all-reduce | flops 2 | bytes 16 | tf_op jit(solution)/shard_map/psum | solution.py:15
  160.6 3.4 %all-reduce.3 = (f32[]{:T(128)}, f32[]{:T(128)}) all-reduce(f32[]{:T(128)} %get-tuple-element.20, f32[]{:T(128)} %get-tuple-element.21), channel_id=1, replica_groups=mesh['grp_0'=8,'grp_1'=4,'rep_0'=4,'rep_1'=2] {'rep_1'}, use_global_device_ids=true, to_apply=%region_14.16 | all-reduce | flops 2 | bytes 16 | tf_op jit(solution)/shard_map/psum | solution.py:15
  165.9 14.0 %all_to_all.37 = f32[32,1,8]{2,1,0:T(1,128)S(1)} all-to-all(f32[32,1,8]{2,1,0:T(1,128)S(1)} %bitcast.76), channel_id=1, replica_groups=mesh['grp_0'=8,'grp_1'=4,'rep_0'=4,'rep_1'=2] {'grp_0','grp_1'}, dimensions={0} | all-to-all | bytes 2048 | tf_op jit(solution)/shard_map/all_to_all | solution.py:117
  180.7 10.3 %convolution_convert_fusion.4 = bf16[256,32,128]{2,1,0:T(8,128)(2,1)} fusion(bf16[256,180,128]{2,1,0:T(8,128)(2,1)} %copy.32, f32[256,32,180]{2,1,0:T(8,128)} %get-tuple-element.29, f32[256,32]{1,0:T(8,128)S(1)} %fusion.2, f32[256]{0:T(256)S(1)} %mul.78, f32[256,32]{1,0:T(8,128)S(1)} %get-tuple-element.28, s32[256]{0:T(256)S(1)} %fusion.14), kind=kOutput, calls=%fused_computation.18 | convolution fusion | flops 390332416 | bytes 19859456 | tf_op jit(solution)/shard_map/sij,sjd->sid/dot_general | solution.py:121
  191.0 4.2 %reshape.248 = bf16[32,8,4096]{2,1,0:T(8,128)(2,1)} reshape(bf16[256,32,128]{2,1,0:T(8,128)(2,1)} %convolution_convert_fusion.4) | data formatting | bytes 4194304 | tf_op jit(solution)/shard_map/reshape | solution.py:125
  195.2 5.8 %all-to-all-start.4 = ((bf16[32,8,4096]{2,1,0:T(8,128)(2,1)}), bf16[32,8,4096]{2,1,0:T(8,128)(2,1)}, u32[]{:S(2)}, u32[]{:S(2)}) async-start(bf16[32,8,4096]{2,1,0:T(8,128)(2,1)} %reshape.248), calls=%async_computation.4 | async-start | bytes 4194304 | tf_op jit(solution)/shard_map/all_to_all | solution.py:124
  202.5 14.7 %convolution_convert_fusion.2 = bf16[256,180,128]{2,1,0:T(8,128)(2,1)} fusion(bf16[256,32,128]{2,1,0:T(8,128)(2,1)S(1)} %bitcast.74, f32[256,32,180]{2,1,0:T(8,128)} %get-tuple-element.29, f32[256,32]{1,0:T(8,128)S(1)} %fusion.2, f32[256]{0:T(256)S(1)} %mul.78, f32[256,32]{1,0:T(8,128)S(1)} %get-tuple-element.28, s32[256]{0:T(256)S(1)} %fusion.14), kind=kOutput, calls=%fused_computation.11 | convolution fusion | flops 395182080 | bytes 19859456 | tf_op jit(solution)/shard_map/sij,sid->sjd/dot_general | solution.py:137
  217.2 16.4 %copy.37 = bf16[256,180,128]{0,2,1:T(8,128)(2,1)} copy(bf16[256,180,128]{2,1,0:T(8,128)(2,1)} %convolution_convert_fusion.2) | data formatting | bytes 23592960 | tf_op jit(solution)/shard_map/convert_element_type | solution.py:139
  233.6 8.0 %convolution_convert_fusion.1 = bf16[64,23040]{1,0:T(8,128)(2,1)S(1)} fusion(bf16[256,23040]{0,1:T(8,128)(2,1)} %bitcast.69, s32[256]{0:T(256)S(1)} %reshape.239), kind=kOutput, calls=%fused_computation.6 | convolution fusion | flops 756465664 | bytes 14746624 | tf_op jit(solution)/shard_map/dot_general | solution.py:141
  244.5 4.2 %copy.38 = bf16[64,1,180,128]{3,0,2,1:T(8,128)(2,1)} copy(bf16[64,1,180,128]{3,2,0,1:T(8,128)(2,1)} %reshape.251) | data formatting | bytes 5898240
  250.8 3.3 %copy.36 = bf16[256,4096]{0,1:T(8,128)(2,1)S(1)} copy(bf16[256,4096]{1,0:T(8,128)(2,1)} %bitcast.18) | data formatting | bytes 4194304 | tf_op jit(solution)/shard_map/reshape | solution.py:133
  (64 shorter events, 30.4 us)
Async XLA Ops:
  0.6 16.9 %copy-start = (bf16[2,1,32,128]{3,2,1,0:T(8,128)(2,1)S(1)}, bf16[2,1,32,128]{3,2,1,0:T(8,128)(2,1)}, u32[]{:S(2)}) copy-start(bf16[2,1,32,128]{3,2,1,0:T(8,128)(2,1)} %param.8) | copy-start | bytes 49156
  0.6 34.8 %copy-start.3 = (f32[2,1,64]{2,1,0:T(1,128)S(1)}, f32[2,1,64]{2,1,0:T(1,128)}, u32[]{:S(2)}) copy-start(f32[2,1,64]{2,1,0:T(1,128)} %param.13) | copy-start | bytes 1540
  5.7 20.2 %all-to-all-start = ((s32[32,1,8]{2,1,0:T(1,128)}), s32[32,1,8]{2,1,0:T(1,128)S(1)}, u32[]{:S(2)}, u32[]{:S(2)}) async-start(s32[32,1,8]{2,1,0:T(1,128)} %bitcast.6), calls=%async_computation | async-start | bytes 32768 | tf_op jit(solution)/shard_map/all_to_all | solution.py:61
  25.9 54.4 %all-to-all-start.1 = ((bf16[32,8,4096]{2,1,0:T(8,128)(2,1)}), bf16[32,8,4096]{2,1,0:T(8,128)(2,1)}, u32[]{:S(2)}, u32[]{:S(2)}) async-start(bf16[32,8,4096]{2,1,0:T(8,128)(2,1)} %fusion.1), calls=%async_computation.1 | async-start | bytes 4194304 | tf_op jit(solution)/shard_map/all_to_all | solution.py:84
  59.1 16.5 %copy-start.2 = (s32[64,1]{0,1:T(1,128)S(1)}, s32[64,1]{0,1:T(1,128)}, u32[]{:S(2)}) copy-start(s32[64,1]{0,1:T(1,128)} %param.10) | copy-start | bytes 772
  97.6 14.4 %copy-start.4 = (f32[2,1]{0,1:T(1,128)S(1)}, f32[2,1]{0,1:T(1,128)}, u32[]{:S(2)}) copy-start(f32[2,1]{0,1:T(1,128)} %param.14) | copy-start | bytes 28
  104.9 15.6 %all-to-all-start.2 = ((f32[32,1,8]{2,1,0:T(1,128)}), f32[32,1,8]{2,1,0:T(1,128)S(1)}, u32[]{:S(2)}, u32[]{:S(2)}) async-start(f32[32,1,8]{2,1,0:T(1,128)} %bitcast.12), calls=%async_computation.2 | async-start | bytes 32768 | tf_op jit(solution)/shard_map/all_to_all | solution.py:96
  195.2 55.6 %all-to-all-start.4 = ((bf16[32,8,4096]{2,1,0:T(8,128)(2,1)}), bf16[32,8,4096]{2,1,0:T(8,128)(2,1)}, u32[]{:S(2)}, u32[]{:S(2)}) async-start(bf16[32,8,4096]{2,1,0:T(8,128)(2,1)} %reshape.248), calls=%async_computation.4 | async-start | bytes 4194304 | tf_op jit(solution)/shard_map/all_to_all | solution.py:124
  233.6 21.9 %copy-start.1 = (bf16[2,1,32,128]{3,2,1,0:T(8,128)(2,1)S(1)}, bf16[2,1,32,128]{3,2,1,0:T(8,128)(2,1)}, u32[]{:S(2)}) copy-start(bf16[2,1,32,128]{3,2,1,0:T(8,128)(2,1)} %param.8) | copy-start | bytes 49156
where the time goes:
time: 259 us; the launch traced here: 257 us
  local copies, waits for them, and re-layouts  78.7 us (30%)
  matrix products  58 us (22%)
  blocking collectives  53.7 us (21%)
  starting transfers between devices  30.4 us (12%)
  waiting for transfers between devices  18.2 us (7%)
  other arithmetic  14.3 us (6%)
  between operations  3.42 us (1%)
    psum x4, blocking collectives, over_axes(): shard = lax.psum(shard, axis)  39.6 us
    reshape x1, local copies, waits for them, and re-layouts, on_device(): blocks = blocks_flat.reshape(slot_count, token_len, feature_dim)  16.5 us
    convert_element_type x1, local copies, waits for them, and re-layouts, on_device(): returned = jnp.einsum('sij,sid->sjd', scaled_grad, got_queries, preferred...  16.4 us
    convert_element_type x1, local copies, waits for them, and re-layouts, on_device(): jnp.dot(pick_hot, flat_passages, preferred_element_type=jnp.float32)  16.2 us
    dot_general x1, matrix products, on_device(): jnp.einsum('sid,sjd->sij', got_queries, blocks, preferred_element_type=jn...  15.2 us
    dot_general x1, matrix products, on_device(): jnp.einsum('sij,sid->sjd', scaled_grad, got_queries, preferred_element_ty...  14.7 us
    all_to_all x1, blocking collectives, on_device(): lax.all_to_all(slot_score_grad.reshape(groups, capacity), GRP, split_axis...  14 us
    all_to_all x1, starting transfers between devices, on_device(): lax.all_to_all(request.reshape(groups, capacity), GRP, split_axis=0, conc...  11.7 us
  transfers between devices with their start and end apart: 4, of which 4 were waited for; matrix products, arithmetic and copies ran while one was open for 37% of the time, Pallas kernels for 0%

commit v1 on v0

--- a/solution.py
+++ b/solution.py
@@ -12,7 +12,7 @@
 
 def over_axes(shard, axes):
     for axis in axes:
-        shard = lax.psum(shard, axis)
+        shard = jnp.sum(lax.all_gather(shard, axis), axis=0)
     return shard
 
 

time: 259 us -> 272 us (1.050)
  local copies, waits for them, and re-layouts: 78.7 us -> 92.5 us
  other arithmetic: 14.3 us -> 19.3 us
  blocking collectives: 53.7 us -> 50.8 us
    psum x4 -> x0, blocking collectives: 39.6 us -> none  [over_axes(): shard = lax.psum(shard, axis)]
    unnamed x0 -> x4, blocking collectives: none -> 36.8 us
    unnamed x14 -> x42, local copies, waits for them, and re-layouts: 10.6 us -> 24.4 us
    reduce_sum x0 -> x8, other arithmetic: none -> 5.05 us  [over_axes(): shard = jnp.sum(lax.all_gather(shard, axis), axis=0)]
  transfers between devices with their start and end apart: 4 -> 4, of which waited for: 4 -> 4; matrix products, arithmetic and copies ran while one was open for 37% -> 36% of each run, Pallas kernels for 0% -> 0%
where the time goes in v1:
time: 272 us; the launch traced here: 270 us
  local copies, waits for them, and re-layouts  92.5 us (34%)
  matrix products  58 us (21%)
  blocking collectives  50.8 us (19%)
  starting transfers between devices  30.4 us (11%)
  other arithmetic  19.3 us (7%)
  waiting for transfers between devices  15.6 us (6%)
  between operations  3.44 us (1%)
    unnamed x4, blocking collectives  36.8 us
    unnamed x42, local copies, waits for them, and re-layouts  24.4 us
    reshape x1, local copies, waits for them, and re-layouts, on_device(): blocks = blocks_flat.reshape(slot_count, token_len, feature_dim)  16.5 us
    convert_element_type x1, local copies, waits for them, and re-layouts, on_device(): returned = jnp.einsum('sij,sid->sjd', scaled_grad, got_queries, preferred...  16.4 us
    convert_element_type x1, local copies, waits for them, and re-layouts, on_device(): jnp.dot(pick_hot, flat_passages, preferred_element_type=jnp.float32)  16.2 us
    dot_general x1, matrix products, on_device(): jnp.einsum('sid,sjd->sij', got_queries, blocks, preferred_element_type=jn...  15.2 us
    dot_general x1, matrix products, on_device(): jnp.einsum('sij,sid->sjd', scaled_grad, got_queries, preferred_element_ty...  14.7 us
    all_to_all x1, blocking collectives, on_device(): lax.all_to_all(slot_score_grad.reshape(groups, capacity), GRP, split_axis...  14 us
  transfers between devices with their start and end apart: 4, of which 4 were waited for; matrix products, arithmetic and copies ran while one was open for 36% of the time, Pallas kernels for 0%

profile of v1, /device:TPU:8, one launch (start us, length us, event | category | flops | bytes accessed | tf_op | source)
XLA Modules:
  0.0 270.1 jit_solution(5656412660040730990)
XLA Ops:
  5.7 11.7 %all-to-all-start = ((s32[32,1,8]{2,1,0:T(1,128)}), s32[32,1,8]{2,1,0:T(1,128)S(1)}, u32[]{:S(2)}, u32[]{:S(2)}) async-start(s32[32,1,8]{2,1,0:T(1,128)} %bitcast.6), calls=%async_computation | async-start | bytes 32768 | tf_op jit(solution)/shard_map/all_to_all | solution.py:61
  20.4 5.5 %all-to-all-done = s32[32,1,8]{2,1,0:T(1,128)S(1)} async-done(((s32[32,1,8]{2,1,0:T(1,128)}), s32[32,1,8]{2,1,0:T(1,128)S(1)}, u32[]{:S(2)}, u32[]{:S(2)}) %all-to-all-start) | async-done | bytes 1056 | tf_op jit(solution)/shard_map/all_to_all | solution.py:61
  25.9 5.8 %all-to-all-start.1 = ((bf16[32,8,4096]{2,1,0:T(8,128)(2,1)}), bf16[32,8,4096]{2,1,0:T(8,128)(2,1)}, u32[]{:S(2)}, u32[]{:S(2)}) async-start(bf16[32,8,4096]{2,1,0:T(8,128)(2,1)} %fusion.1), calls=%async_computation.1 | async-start | bytes 4194304 | tf_op jit(solution)/shard_map/all_to_all | solution.py:84
  31.7 3.7 %copy.30 = bf16[64,1,180,128]{3,2,0,1:T(8,128)(2,1)S(1)} copy(bf16[64,1,180,128]{3,0,2,1:T(8,128)(2,1)} %param.9) | data formatting | bytes 5898240 | tf_op args[1]
  36.7 6.2 %convolution_convert_fusion = bf16[256,23040]{1,0:T(8,128)(2,1)} fusion(bf16[8,8,180,128]{3,2,1,0:T(8,128)(2,1)S(1)} %bitcast.83, s32[256]{0:T(256)S(1)} %reshape.239), kind=kOutput, calls=%fused_computation.5 | convolution fusion | flops 760889344 | bytes 14746624 | tf_op jit(solution)/shard_map/dot_general | solution.py:77
  42.9 16.2 %copy.31 = bf16[256,23040]{0,1:T(8,128)(2,1)} copy(bf16[256,23040]{1,0:T(8,128)(2,1)} %convolution_convert_fusion) | data formatting | bytes 23592960 | tf_op jit(solution)/shard_map/convert_element_type | solution.py:77
  59.1 16.5 %copy.32 = bf16[256,180,128]{2,1,0:T(8,128)(2,1)} copy(bf16[256,180,128]{0,2,1:T(8,128)(2,1)} %bitcast.82) | data formatting | bytes 23592960 | tf_op jit(solution)/shard_map/reshape | solution.py:92
  82.4 15.2 %fusion = (f32[256,32]{1,0:T(8,128)S(1)}, f32[256,32,180]{2,1,0:T(8,128)}) fusion(s32[256]{0:T(256)S(1)} %fusion.14, bf16[256,32,128]{2,1,0:T(8,128)(2,1)S(1)} %bitcast.85, bf16[256,180,128]{2,1,0:T(8,128)(2,1)} %copy.32), kind=kOutput, calls=%fused_computation.12 | convolution fusion | flops 383377408 | bytes 19825664 | tf_op jit(solution)/shard_map/sid,sjd->sij/dot_general | solution.py:93
  97.7 6.5 %fusion.2 = f32[256,32]{1,0:T(8,128)S(1)} fusion(f32[256,32,180]{2,1,0:T(8,128)} %get-tuple-element.29, f32[256,32]{1,0:T(8,128)S(1)} %get-tuple-element.28, s32[256]{0:T(256)S(1)} %fusion.14), kind=kLoop, calls=%fused_computation.15 | loop fusion | flops 8839168 | bytes 5964800 | tf_op jit(solution)/shard_map/reduce_sum | solution.py:27
  105.0 7.1 %all-to-all-start.2 = ((f32[32,1,8]{2,1,0:T(1,128)}), f32[32,1,8]{2,1,0:T(1,128)S(1)}, u32[]{:S(2)}, u32[]{:S(2)}) async-start(f32[32,1,8]{2,1,0:T(1,128)} %bitcast.12), calls=%async_computation.2 | async-start | bytes 32768 | tf_op jit(solution)/shard_map/all_to_all | solution.py:96
  114.8 5.8 %all-to-all-done.2 = f32[32,1,8]{2,1,0:T(1,128)S(1)} async-done(((f32[32,1,8]{2,1,0:T(1,128)}), f32[32,1,8]{2,1,0:T(1,128)S(1)}, u32[]{:S(2)}, u32[]{:S(2)}) %all-to-all-start.2) | async-done | bytes 1056 | tf_op jit(solution)/shard_map/all_to_all | solution.py:96
  126.5 14.7 %all-reduce.8 = (f32[8]{0:T(128)S(1)}, f32[8]{0:T(128)S(1)}) all-reduce(f32[8]{0:T(128)S(1)} %dynamic-update-slice, f32[8]{0:T(128)S(1)} %dynamic-update-slice.4), channel_id=1, replica_groups=mesh['grp_0'=8,'grp_1'=4,'rep_0'=4,'rep_1'=2] {'grp_0'}, use_global_device_ids=true, to_apply=%add | all-reduce | flops 16 | bytes 128
  146.0 9.2 %all-reduce.10 = (f32[4]{0:T(128)S(1)}, f32[4]{0:T(128)S(1)}) all-reduce(f32[4]{0:T(128)S(1)} %dynamic-update-slice.1, f32[4]{0:T(128)S(1)} %dynamic-update-slice.5), channel_id=1, replica_groups=mesh['grp_0'=8,'grp_1'=4,'rep_0'=4,'rep_1'=2] {'grp_1'}, use_global_device_ids=true, to_apply=%add.1 | all-reduce | flops 8 | bytes 64
  159.9 10.4 %all-reduce.9 = (f32[4]{0:T(128)S(1)}, f32[4]{0:T(128)S(1)}) all-reduce(f32[4]{0:T(128)S(1)} %dynamic-update-slice.2, f32[4]{0:T(128)S(1)} %dynamic-update-slice.6), channel_id=1, replica_groups=mesh['grp_0'=8,'grp_1'=4,'rep_0'=4,'rep_1'=2] {'rep_0'}, use_global_device_ids=true, to_apply=%add.2 | all-reduce | flops 8 | bytes 64
  179.4 14.0 %all_to_all.37 = f32[32,1,8]{2,1,0:T(1,128)S(1)} all-to-all(f32[32,1,8]{2,1,0:T(1,128)S(1)} %bitcast.88), channel_id=1, replica_groups=mesh['grp_0'=8,'grp_1'=4,'rep_0'=4,'rep_1'=2] {'grp_0','grp_1'}, dimensions={0} | all-to-all | bytes 2048 | tf_op jit(solution)/shard_map/all_to_all | solution.py:117
  194.2 10.3 %convolution_convert_fusion.4 = bf16[256,32,128]{2,1,0:T(8,128)(2,1)} fusion(bf16[256,180,128]{2,1,0:T(8,128)(2,1)} %copy.32, f32[256,32,180]{2,1,0:T(8,128)} %get-tuple-element.29, f32[256,32]{1,0:T(8,128)S(1)} %fusion.2, f32[256]{0:T(256)S(1)} %mul.78, f32[256,32]{1,0:T(8,128)S(1)} %get-tuple-element.28, s32[256]{0:T(256)S(1)} %fusion.14), kind=kOutput, calls=%fused_computation.18 | convolution fusion | flops 390332416 | bytes 19859456 | tf_op jit(solution)/shard_map/sij,sjd->sid/dot_general | solution.py:121
  204.5 4.2 %reshape.248 = bf16[32,8,4096]{2,1,0:T(8,128)(2,1)} reshape(bf16[256,32,128]{2,1,0:T(8,128)(2,1)} %convolution_convert_fusion.4) | data formatting | bytes 4194304 | tf_op jit(solution)/shard_map/reshape | solution.py:125
  208.7 5.8 %all-to-all-start.4 = ((bf16[32,8,4096]{2,1,0:T(8,128)(2,1)}), bf16[32,8,4096]{2,1,0:T(8,128)(2,1)}, u32[]{:S(2)}, u32[]{:S(2)}) async-start(bf16[32,8,4096]{2,1,0:T(8,128)(2,1)} %reshape.248), calls=%async_computation.4 | async-start | bytes 4194304 | tf_op jit(solution)/shard_map/all_to_all | solution.py:124
  216.6 14.7 %convolution_convert_fusion.2 = bf16[256,180,128]{2,1,0:T(8,128)(2,1)} fusion(bf16[256,32,128]{2,1,0:T(8,128)(2,1)S(1)} %bitcast.86, f32[256,32,180]{2,1,0:T(8,128)} %get-tuple-element.29, f32[256,32]{1,0:T(8,128)S(1)} %fusion.2, f32[256]{0:T(256)S(1)} %mul.78, f32[256,32]{1,0:T(8,128)S(1)} %get-tuple-element.28, s32[256]{0:T(256)S(1)} %fusion.14), kind=kOutput, calls=%fused_computation.11 | convolution fusion | flops 395182080 | bytes 19859456 | tf_op jit(solution)/shard_map/sij,sid->sjd/dot_general | solution.py:137
  231.2 16.4 %copy.37 = bf16[256,180,128]{0,2,1:T(8,128)(2,1)} copy(bf16[256,180,128]{2,1,0:T(8,128)(2,1)} %convolution_convert_fusion.2) | data formatting | bytes 23592960 | tf_op jit(solution)/shard_map/convert_element_type | solution.py:139
  247.6 8.0 %convolution_convert_fusion.1 = bf16[64,23040]{1,0:T(8,128)(2,1)S(1)} fusion(bf16[256,23040]{0,1:T(8,128)(2,1)} %bitcast.81, s32[256]{0:T(256)S(1)} %reshape.239), kind=kOutput, calls=%fused_computation.6 | convolution fusion | flops 756465664 | bytes 14746624 | tf_op jit(solution)/shard_map/dot_general | solution.py:141
  255.7 2.9 %reshape.251 = bf16[64,1,180,128]{3,2,0,1:T(8,128)(2,1)} reshape(bf16[64,23040]{1,0:T(8,128)(2,1)S(1)} %convolution_convert_fusion.1) | data formatting | bytes 5898240 | tf_op jit(solution)/shard_map/reshape | solution.py:142
  258.5 4.2 %copy.38 = bf16[64,1,180,128]{3,0,2,1:T(8,128)(2,1)} copy(bf16[64,1,180,128]{3,2,0,1:T(8,128)(2,1)} %reshape.251) | data formatting | bytes 5898240
  264.3 3.3 %copy.36 = bf16[256,4096]{0,1:T(8,128)(2,1)S(1)} copy(bf16[256,4096]{1,0:T(8,128)(2,1)} %bitcast.30) | data formatting | bytes 4194304 | tf_op jit(solution)/shard_map/reshape | solution.py:133
  (100 shorter events, 48.3 us)
Async XLA Ops:
  0.6 16.9 %copy-start = (bf16[2,1,32,128]{3,2,1,0:T(8,128)(2,1)S(1)}, bf16[2,1,32,128]{3,2,1,0:T(8,128)(2,1)}, u32[]{:S(2)}) copy-start(bf16[2,1,32,128]{3,2,1,0:T(8,128)(2,1)} %param.8) | copy-start | bytes 49156
  0.6 34.8 %copy-start.3 = (f32[2,1,64]{2,1,0:T(1,128)S(1)}, f32[2,1,64]{2,1,0:T(1,128)}, u32[]{:S(2)}) copy-start(f32[2,1,64]{2,1,0:T(1,128)} %param.13) | copy-start | bytes 1540
  5.7 20.2 %all-to-all-start = ((s32[32,1,8]{2,1,0:T(1,128)}), s32[32,1,8]{2,1,0:T(1,128)S(1)}, u32[]{:S(2)}, u32[]{:S(2)}) async-start(s32[32,1,8]{2,1,0:T(1,128)} %bitcast.6), calls=%async_computation | async-start | bytes 32768 | tf_op jit(solution)/shard_map/all_to_all | solution.py:61
  25.9 54.4 %all-to-all-start.1 = ((bf16[32,8,4096]{2,1,0:T(8,128)(2,1)}), bf16[32,8,4096]{2,1,0:T(8,128)(2,1)}, u32[]{:S(2)}, u32[]{:S(2)}) async-start(bf16[32,8,4096]{2,1,0:T(8,128)(2,1)} %fusion.1), calls=%async_computation.1 | async-start | bytes 4194304 | tf_op jit(solution)/shard_map/all_to_all | solution.py:84
  59.1 16.5 %copy-start.2 = (s32[64,1]{0,1:T(1,128)S(1)}, s32[64,1]{0,1:T(1,128)}, u32[]{:S(2)}) copy-start(s32[64,1]{0,1:T(1,128)} %param.10) | copy-start | bytes 772
  97.6 14.5 %copy-start.8 = (u32[256]{0:T(256)S(1)}, u32[256]{0:T(256)}, u32[]{:S(2)}) copy-start(u32[256]{0:T(256)} %constant.82) | copy-start | bytes 3076
  97.7 15.1 %copy-start.4 = (f32[2,1]{0,1:T(1,128)S(1)}, f32[2,1]{0,1:T(1,128)}, u32[]{:S(2)}) copy-start(f32[2,1]{0,1:T(1,128)} %param.14) | copy-start | bytes 28
  97.7 28.3 %copy-start.7 = (u32[256]{0:T(256)S(1)}, u32[256]{0:T(256)}, u32[]{:S(2)}) copy-start(u32[256]{0:T(256)} %constant.87) | copy-start | bytes 3076
  97.7 47.7 %copy-start.6 = (u32[256]{0:T(256)S(1)}, u32[256]{0:T(256)}, u32[]{:S(2)}) copy-start(u32[256]{0:T(256)} %constant.92) | copy-start | bytes 3076
  97.7 61.7 %copy-start.5 = (u32[256]{0:T(256)S(1)}, u32[256]{0:T(256)}, u32[]{:S(2)}) copy-start(u32[256]{0:T(256)} %constant.97) | copy-start | bytes 3076
  105.0 15.6 %all-to-all-start.2 = ((f32[32,1,8]{2,1,0:T(1,128)}), f32[32,1,8]{2,1,0:T(1,128)S(1)}, u32[]{:S(2)}, u32[]{:S(2)}) async-start(f32[32,1,8]{2,1,0:T(1,128)} %bitcast.12), calls=%async_computation.2 | async-start | bytes 32768 | tf_op jit(solution)/shard_map/all_to_all | solution.py:96
  208.7 55.6 %all-to-all-start.4 = ((bf16[32,8,4096]{2,1,0:T(8,128)(2,1)}), bf16[32,8,4096]{2,1,0:T(8,128)(2,1)}, u32[]{:S(2)}, u32[]{:S(2)}) async-start(bf16[32,8,4096]{2,1,0:T(8,128)(2,1)} %reshape.248), calls=%async_computation.4 | async-start | bytes 4194304 | tf_op jit(solution)/shard_map/all_to_all | solution.py:124
  247.6 21.4 %copy-start.1 = (bf16[2,1,32,128]{3,2,1,0:T(8,128)(2,1)S(1)}, bf16[2,1,32,128]{3,2,1,0:T(8,128)(2,1)}, u32[]{:S(2)}) copy-start(bf16[2,1,32,128]{3,2,1,0:T(8,128)(2,1)} %param.8) | copy-start | bytes 49156
